TPU v7x, 32 devices: a whole 2x2x4 slice. The times are simulated.
32 devices in a mesh: lat: 2 (over core), lon: 2 (over y), lev: 2 (over x), unit: 4 (over z).
Axes of the slice: x: 2, y: 2, z: 4, core: 2. Of those that a mesh axis runs over, the one named last changes fastest.
Arguments:
- tracer: float32 [32, 256, 32, 128], P(('unit', 'lat'), 'lon', 'lev'), parts along dimension 0, may hold values from 0.5 to 2
- diffusivity: float32 [32, 256, 32, 128], P(('unit', 'lat'), 'lon', 'lev'), parts along dimension 0, may hold values from 0.03 to 0.15
- source: float32 [32, 256, 32, 128], P(('unit', 'lat'), 'lon', 'lev'), parts along dimension 0, may hold values from -0.2 to 0.2
Outputs:
- standardized: float32 [32, 256, 32, 128], P(('unit', 'lat'), 'lon', 'lev'), parts along dimension 0
- tracer_end: float32 [32, 256, 32, 128], P(('unit', 'lat'), 'lon', 'lev'), parts along dimension 0
There are 4 independent parts, one for each index of `unit`. A program takes and returns all parts, laid end to end along the dimension named above; each array names one. Nothing has to cross between parts.
All inputs are finite; a program needn't handle non-finite values.
Results may differ from a plain program's by a relative error of at most 0.00002.
Values sent between devices are 32-bit elements; how exact they have to be, the bound alone decides.
A program may use at most 128 MiB of HBM per device.

v0:
```python
import functools

import jax
import jax.numpy as jnp
from jax import lax
from jax.experimental import pallas as pl
from jax.experimental.pallas import tpu as pltpu
from jax.sharding import PartitionSpec as P

STEPS = 4
PAD = 8
EPSILON = 0.0001
MESH = pl.DeviceIdType.MESH


def rows_of(extent):
    for rows in (32, 16, 8):
        if extent % rows == 0:
            return rows
    return extent


def steps_kernel(
    sizes, shape, tracer, diffusivity, source, standardized, tracer_end,
    field, coeff, forcing, last, own, others,
    load_sem, lev_send, lev_recv, lat_send, lat_recv, lon_send, lon_recv, stat_send, stat_recv,
):
    n_j, n_i, n_k, _ = shape
    n_lat, n_lon, n_lev = sizes
    inner = pl.ds(PAD, n_i)
    whole_j = pl.ds(1, n_j)
    chunk = rows_of(n_i)
    lat, lon, lev = lax.axis_index("lat"), lax.axis_index("lon"), lax.axis_index("lev")
    lat_up, lat_down = lax.rem(lat + 1, n_lat), lax.rem(lat + n_lat - 1, n_lat)
    lon_up, lon_down = lax.rem(lon + 1, n_lon), lax.rem(lon + n_lon - 1, n_lon)
    lev_up, lev_down = lax.rem(lev + 1, n_lev), lax.rem(lev + n_lev - 1, n_lev)

    def load(which, k):
        array = (tracer, diffusivity, source)[which]
        if which == 0:
            target = field.at[0, k + 1, whole_j, inner, :]
        else:
            target = (coeff, forcing)[which - 1].at[k]
        return pltpu.make_async_copy(array.at[:, :, k, :], target, load_sem.at[which, k])

    def remote(src, dst, send, recv, device):
        return pltpu.make_async_remote_copy(
            src_ref=src, dst_ref=dst, send_sem=send, recv_sem=recv,
            device_id=device, device_id_type=MESH,
        )

    def lev_copies(step, j):
        down = remote(
            field.at[step, 1, j, inner, :], field.at[step, n_k + 1, j, inner, :],
            lev_send.at[step, j - 1, 0], lev_recv.at[step, j - 1, 0], {"lev": lev_down},
        )
        up = remote(
            field.at[step, n_k, j, inner, :], field.at[step, 0, j, inner, :],
            lev_send.at[step, j - 1, 1], lev_recv.at[step, j - 1, 1], {"lev": lev_up},
        )
        return down, up

    parts = (pl.ds(1, 1), pl.ds(n_k, 1), pl.ds(2, n_k - 2))

    def lat_copy(step, part, side):
        k = parts[part]
        src, dst, to = ((1, n_j + 1, lat_down), (n_j, 0, lat_up))[side]
        return remote(
            field.at[step, k, src, inner, :], field.at[step, k, dst, inner, :],
            lat_send.at[step, part, side], lat_recv.at[step, part, side], {"lat": to},
        )

    def lon_copy(step, part, side):
        k = parts[part]
        src, dst, to = (
            (PAD, PAD + n_i, lon_down), (PAD + n_i - 1, PAD - 1, lon_up)
        )[side]
        return remote(
            field.at[step, k, whole_j, pl.ds(src, 1), :],
            field.at[step, k, whole_j, pl.ds(dst, 1), :],
            lon_send.at[step, part, side], lon_recv.at[step, part, side], {"lon": to},
        )

    def stat_copies(j):
        return [
            remote(
                own.at[j - 1], others.at[n_lev - 1 - away, j - 1],
                stat_send.at[away - 1, j - 1], stat_recv.at[n_lev - 1 - away, j - 1],
                {"lev": lax.rem(lev + away, n_lev)},
            )
            for away in range(1, n_lev)
        ]

    def update(step, k, j):
        for low in range(0, n_i, chunk):
            r = PAD + low
            middle = field[step, k, j, pl.ds(r, chunk), :]
            spread = (
                field[step, k, j - 1, pl.ds(r, chunk), :] + field[step, k, j + 1, pl.ds(r, chunk), :]
                + field[step, k, j, pl.ds(r - 1, chunk), :] + field[step, k, j, pl.ds(r + 1, chunk), :]
                + field[step, k - 1, j, pl.ds(r, chunk), :] + field[step, k + 1, j, pl.ds(r, chunk), :]
                - 6.0 * middle
            )
            rows = pl.ds(low, chunk)
            value = middle + coeff[k - 1, j - 1, rows, :] * spread + forcing[k - 1, j - 1, rows, :]
            if step == STEPS - 1:
                last[k - 1, j - 1, rows, :] = value
                place = pl.ds(low * n_k + k - 1, chunk, stride=n_k)
                tracer_end[j - 1, place, :] = value
            else:
                field[step + 1, k, j, pl.ds(r, chunk), :] = value

    def summarise(j):
        for low in range(0, n_i, chunk):
            rows = pl.ds(low, chunk)
            total = last[0, j - 1, rows, :]
            for k in range(1, n_k):
                total = total + last[k, j - 1, rows, :]
            mean = total * (1.0 / n_k)
            squares = jnp.zeros_like(mean)
            for k in range(n_k):
                moved = last[k, j - 1, rows, :] - mean
                squares = squares + moved * moved
            own[j - 1, 0, rows, :] = mean
            own[j - 1, 1, rows, :] = squares

    def combine(j):
        for low in range(0, n_i, chunk):
            rows = pl.ds(low, chunk)
            means = [own[j - 1, 0, rows, :]] + [others[p, j - 1, 0, rows, :] for p in range(n_lev - 1)]
            mean = functools.reduce(jnp.add, means) * (1.0 / n_lev)
            squares = own[j - 1, 1, rows, :]
            for p in range(n_lev - 1):
                squares = squares + others[p, j - 1, 1, rows, :]
            for part in means:
                squares = squares + n_k * ((part - mean) * (part - mean))
            scale = lax.rsqrt(squares * (1.0 / (n_k * n_lev)) + EPSILON)
            for k in range(n_k):
                place = pl.ds(low * n_k + k, chunk, stride=n_k)
                standardized[j - 1, place, :] = (last[k, j - 1, rows, :] - mean) * scale

    def over_k(first, end, body):
        def wrapped(k, carry):
            body(k)
            return carry
        lax.fori_loop(first, end, wrapped, 0)

    edges = (0, n_k - 1)
    for k in edges:
        load(0, k).start()

    barrier = pltpu.get_barrier_semaphore()
    greeted = (
        [{"lat": lax.rem(lat + a, n_lat)} for a in sorted({1, n_lat - 1})]
        + [{"lon": lax.rem(lon + a, n_lon)} for a in sorted({1, n_lon - 1})]
        + [{"lev": lax.rem(lev + a, n_lev)} for a in range(1, n_lev)]
    )
    for device in greeted:
        pl.semaphore_signal(barrier, inc=1, device_id=device, device_id_type=MESH)
    pl.semaphore_wait(barrier, len(greeted))

    for k in edges:
        load(0, k).wait()
    for j in range(1, n_j + 1):
        for copy in lev_copies(0, j):
            copy.start()
    for k in (1, n_k - 2):
        load(0, k).start()
    for which in (1, 2):
        for k in edges:
            load(which, k).start()
    over_k(2, n_k - 2, lambda k: load(0, k).start())
    for which in (1, 2):
        over_k(1, n_k - 1, lambda k: load(which, k).start())
    for part in (0, 1):
        for side in (0, 1):
            lat_copy(0, part, side).start()
            lon_copy(0, part, side).start()
    for k in (1, n_k - 2):
        load(0, k).wait()
    for which in (1, 2):
        for k in edges:
            load(which, k).wait()

    def inside(step):
        for side in (0, 1):
            lat_copy(step, 2, side).wait_recv()
            lon_copy(step, 2, side).wait_recv()

        def body(k):
            def across(j, carry):
                update(step, k, j)
                return carry
            lax.fori_loop(1, n_j + 1, across, 0)

        over_k(2, n_k, body)
        if step < STEPS - 1:
            for side in (0, 1):
                lat_copy(step + 1, 2, side).start()
                lon_copy(step + 1, 2, side).start()

    def outside(step):
        for part in (0, 1):
            for side in (0, 1):
                lat_copy(step, part, side).wait_recv()
                lon_copy(step, part, side).wait_recv()
        for j in range(1, n_j + 1):
            for copy in lev_copies(step, j):
                copy.wait_recv()
            update(step, 1, j)
            update(step, n_k, j)
            if step < STEPS - 1:
                for copy in lev_copies(step + 1, j):
                    copy.start()
                for side, edge in ((0, 1), (1, n_j)):
                    if j == edge:
                        for part in (0, 1):
                            lat_copy(step + 1, part, side).start()
            else:
                summarise(j)
                for copy in stat_copies(j):
                    copy.start()
        if step < STEPS - 1:
            for part in (0, 1):
                for side in (0, 1):
                    lon_copy(step + 1, part, side).start()

    over_k(2, n_k - 2, lambda k: load(0, k).wait())
    for side in (0, 1):
        lat_copy(0, 2, side).start()
        lon_copy(0, 2, side).start()
    outside(0)
    for which in (1, 2):
        over_k(1, n_k - 1, lambda k: load(which, k).wait())
    inside(0)
    for step in range(1, STEPS):
        inside(step)
        outside(step)
    for j in range(1, n_j + 1):
        for copy in stat_copies(j):
            copy.wait_recv()
        combine(j)

    for step in range(STEPS):
        for j in range(1, n_j + 1):
            for copy in lev_copies(step, j):
                copy.wait_send()
        for part in range(3):
            for side in (0, 1):
                lat_copy(step, part, side).wait_send()
                lon_copy(step, part, side).wait_send()
    for j in range(1, n_j + 1):
        for copy in stat_copies(j):
            copy.wait_send()


def write_kernel(first, second, first_out, second_out, sem):
    copies = [
        pltpu.make_async_copy(src.at[j], dst.at[j], sem.at[which, j])
        for j in range(first.shape[0])
        for which, (src, dst) in enumerate(((first, first_out), (second, second_out)))
    ]
    for copy in copies:
        copy.start()
    for copy in copies:
        copy.wait()


def on_device(sizes, tracer, diffusivity, source):
    shape = tracer.shape
    n_j, n_i, n_k, levels = shape
    n_lev = sizes[2]
    f32 = jnp.float32
    sem = pltpu.SemaphoreType.DMA
    standardized, tracer_end = pl.pallas_call(
        functools.partial(steps_kernel, sizes, shape),
        out_shape=(
            pltpu.VMEM((n_j, n_i * n_k, levels), f32),
            pltpu.VMEM((n_j, n_i * n_k, levels), f32),
        ),
        in_specs=[pl.BlockSpec(memory_space=pl.ANY)] * 3,
        out_specs=(pl.BlockSpec(memory_space=pltpu.VMEM),) * 2,
        scratch_shapes=[
            pltpu.VMEM((STEPS, n_k + 2, n_j + 2, n_i + 2 * PAD, levels), f32),
            pltpu.VMEM((n_k, n_j, n_i, levels), f32),
            pltpu.VMEM((n_k, n_j, n_i, levels), f32),
            pltpu.VMEM((n_k, n_j, n_i, levels), f32),
            pltpu.VMEM((n_j, 2, n_i, levels), f32),
            pltpu.VMEM((n_lev - 1, n_j, 2, n_i, levels), f32),
            sem((3, n_k)),
            sem((STEPS, n_j, 2)), sem((STEPS, n_j, 2)),
            sem((STEPS, 3, 2)), sem((STEPS, 3, 2)),
            sem((STEPS, 3, 2)), sem((STEPS, 3, 2)),
            sem((n_lev - 1, n_j)), sem((n_lev - 1, n_j)),
        ],
        compiler_params=pltpu.CompilerParams(
            collective_id=0, has_side_effects=True, vmem_limit_bytes=48 * 1024 * 1024,
        ),
    )(tracer, diffusivity, source)
    flat = jax.ShapeDtypeStruct((n_j, n_i * n_k, levels), f32)
    standardized, tracer_end = pl.pallas_call(
        write_kernel,
        out_shape=(flat, flat),
        in_specs=[pl.BlockSpec(memory_space=pltpu.VMEM)] * 2,
        out_specs=(pl.BlockSpec(memory_space=pl.ANY),) * 2,
        scratch_shapes=[sem((2, n_j))],
        compiler_params=pltpu.CompilerParams(vmem_limit_bytes=1024 * 1024),
    )(standardized, tracer_end)
    return standardized.reshape(shape), tracer_end.reshape(shape)


def solution(mesh):
    sizes = (mesh.shape["lat"], mesh.shape["lon"], mesh.shape["lev"])
    spec = P(("unit", "lat"), "lon", "lev", None)
    return jax.shard_map(
        functools.partial(on_device, sizes),
        mesh=mesh,
        in_specs=(spec, spec, spec),
        out_specs=(spec, spec),
        check_vma=False,
    )
```

profile of v0, /device:TPU:0, one launch (start us, length us, event | category | flops | bytes accessed | tf_op | source)
XLA Modules:
  0.0 68.6 jit_solution(2957217257332862924)
XLA Ops:
  0.6 64.6 %shard_map.50 = (f32[4,2048,128]{2,1,0:T(8,128)S(1)}, f32[4,2048,128]{2,1,0:T(8,128)S(1)}) custom-call(f32[4,128,16,128]{3,2,1,0:T(8,128)} %tracer.1, f32[4,128,16,128]{3,2,1,0:T(8,128)} %diffusivity.1, f32[4,128,16,128]{3,2,1,0:T(8,128)} %source.1), custom_call_target="tpu_custom_call" | custom-call | tf_op jit(solution)/shard_map/pallas_call | solution.py:275
  65.3 3.4 %shard_map.51 = (f32[4,2048,128]{2,1,0:T(8,128)}, f32[4,2048,128]{2,1,0:T(8,128)}) custom-call(f32[4,2048,128]{2,1,0:T(8,128)S(1)} %get-tuple-element.6.first, f32[4,2048,128]{2,1,0:T(8,128)S(1)} %get-tuple-element.7.second), custom_call_target="tpu_custom_call" | custom-call | tf_op jit(solution)/shard_map/pallas_call | solution.py:301
where the time goes:
time: 68.8 us; the launch traced here: 68.6 us
  Pallas kernels  68 us (99%)
    pallas_call x1, Pallas kernels, on_device(): pl.pallas_call(functools.partial(steps_kernel, sizes, shape), out_shape=(...  64.6 us
    pallas_call x1, Pallas kernels, on_device(): pl.pallas_call(write_kernel, out_shape=(flat, flat), in_specs=[pl.BlockSp...  3.37 us

commit v1 on v0

--- a/solution.py
+++ b/solution.py
@@ -188,6 +188,10 @@
             lon_copy(step, 2, side).wait_recv()
 
         def body(k):
+            if step == 0:
+                for which in (1, 2):
+                    load(which, k - 1).wait()
+
             def across(j, carry):
                 update(step, k, j)
                 return carry
@@ -229,11 +233,7 @@
     for side in (0, 1):
         lat_copy(0, 2, side).start()
         lon_copy(0, 2, side).start()
-    outside(0)
-    for which in (1, 2):
-        over_k(1, n_k - 1, lambda k: load(which, k).wait())
-    inside(0)
-    for step in range(1, STEPS):
+    for step in range(STEPS):
         inside(step)
         outside(step)
     for j in range(1, n_j + 1):

time: 68.8 us -> 67.8 us (0.985)
  Pallas kernels: 68 us -> 67 us
    pallas_call x1, Pallas kernels: 64.6 us -> 63.6 us  [on_device(): pl.pallas_call(functools.partial(steps_kernel, sizes, shape), out_shape=(...]
where the time goes in v1:
time: 67.8 us; the launch traced here: 67.6 us
  Pallas kernels  67 us (99%)
    pallas_call x1, Pallas kernels, on_device(): pl.pallas_call(functools.partial(steps_kernel, sizes, shape), out_shape=(...  63.6 us
    pallas_call x1, Pallas kernels, on_device(): pl.pallas_call(write_kernel, out_shape=(flat, flat), in_specs=[pl.BlockSp...  3.37 us

profile of v1, /device:TPU:0, one launch (start us, length us, event | category | flops | bytes accessed | tf_op | source)
XLA Modules:
  0.0 67.6 jit_solution(13371182256737500861)
XLA Ops:
  0.6 63.6 %shard_map.50 = (f32[4,2048,128]{2,1,0:T(8,128)S(1)}, f32[4,2048,128]{2,1,0:T(8,128)S(1)}) custom-call(f32[4,128,16,128]{3,2,1,0:T(8,128)} %tracer.1, f32[4,128,16,128]{3,2,1,0:T(8,128)} %diffusivity.1, f32[4,128,16,128]{3,2,1,0:T(8,128)} %source.1), custom_call_target="tpu_custom_call" | custom-call | tf_op jit(solution)/shard_map/pallas_call | solution.py:275
  64.3 3.4 %shard_map.51 = (f32[4,2048,128]{2,1,0:T(8,128)}, f32[4,2048,128]{2,1,0:T(8,128)}) custom-call(f32[4,2048,128]{2,1,0:T(8,128)S(1)} %get-tuple-element.6.first, f32[4,2048,128]{2,1,0:T(8,128)S(1)} %get-tuple-element.7.second), custom_call_target="tpu_custom_call" | custom-call | tf_op jit(solution)/shard_map/pallas_call | solution.py:301

commit v2 on v1

v2 whole, which is shorter than its diff:
```python
import functools

import jax
import jax.numpy as jnp
from jax import lax
from jax.experimental import pallas as pl
from jax.experimental.pallas import tpu as pltpu
from jax.sharding import PartitionSpec as P

STEPS = 4
PAD = 8
EPSILON = 0.0001
MESH = pl.DeviceIdType.MESH


def rows_of(extent):
    for rows in (32, 16, 8):
        if extent % rows == 0:
            return rows
    return extent


def others_near(extent):
    return sorted({1, extent - 1})


def steps_kernel(
    sizes, shape, tracer, diffusivity, source, last, tracer_end, own, others,
    field, coeff, forcing,
    load_sem, lev_send, lev_recv, lat_send, lat_recv, lon_send, lon_recv, stat_send, stat_recv,
):
    n_j, n_i, n_k, _ = shape
    n_lat, n_lon, n_lev = sizes
    inner = pl.ds(PAD, n_i)
    whole_j = pl.ds(1, n_j)
    chunk = rows_of(n_i)
    lat, lon, lev = lax.axis_index("lat"), lax.axis_index("lon"), lax.axis_index("lev")
    lat_up, lat_down = lax.rem(lat + 1, n_lat), lax.rem(lat + n_lat - 1, n_lat)
    lon_up, lon_down = lax.rem(lon + 1, n_lon), lax.rem(lon + n_lon - 1, n_lon)
    lev_up, lev_down = lax.rem(lev + 1, n_lev), lax.rem(lev + n_lev - 1, n_lev)

    def load(which, k, sem):
        array = (tracer, diffusivity, source)[which]
        if which == 0:
            target = field.at[0, k + 1, whole_j, inner, :]
        else:
            target = (coeff, forcing)[which - 1].at[k]
        return pltpu.make_async_copy(array.at[:, :, k, :], target, load_sem.at[sem])

    def wait_for(ref, sem):
        pltpu.make_async_copy(ref, ref, sem).wait()

    def remote(src, dst, send, recv, device):
        return pltpu.make_async_remote_copy(
            src_ref=src, dst_ref=dst, send_sem=send, recv_sem=recv,
            device_id=device, device_id_type=MESH,
        )

    def send_lev(step, j):
        recv = lev_recv.at[step % 2, j - 1]
        for edge, halo, to in ((1, n_k + 1, lev_down), (n_k, 0, lev_up)):
            src = field.at[step, edge, j, inner, :]
            remote(src, field.at[step, halo, j, inner, :], lev_send, recv, {"lev": to}).start()

    def wait_lev(step, j):
        wait_for(field.at[step, pl.ds(0, 2), j, inner, :], lev_recv.at[step % 2, j - 1])

    edges, middle = (pl.ds(1, 1), pl.ds(n_k, 1)), (pl.ds(2, n_k - 2),)

    def send_lat(step, planes, side):
        src, dst, to = ((1, n_j + 1, lat_down), (n_j, 0, lat_up))[side]
        recv = lat_recv.at[step % 2, len(planes) - 1]
        for k in planes:
            remote(
                field.at[step, k, src, inner, :], field.at[step, k, dst, inner, :],
                lat_send, recv, {"lat": to},
            ).start()

    def send_lon(step, planes):
        recv = lon_recv.at[step % 2, len(planes) - 1]
        for src, dst, to in ((PAD, PAD + n_i, lon_down), (PAD + n_i - 1, PAD - 1, lon_up)):
            for k in planes:
                remote(
                    field.at[step, k, whole_j, pl.ds(src, 1), :],
                    field.at[step, k, whole_j, pl.ds(dst, 1), :],
                    lon_send, recv, {"lon": to},
                ).start()

    def wait_sides(step, planes):
        count = 2 if len(planes) == 2 else n_k - 2
        k = pl.ds(1, count)
        wait_for(field.at[step, k, pl.ds(0, 2), inner, :], lat_recv.at[step % 2, len(planes) - 1])
        wait_for(
            field.at[step, k, whole_j, pl.ds(PAD, 2), :], lon_recv.at[step % 2, len(planes) - 1]
        )

    def stat_copies(j):
        return [
            remote(
                own.at[j - 1], others.at[n_lev - 1 - away, j - 1],
                stat_send, stat_recv.at[n_lev - 1 - away, j - 1],
                {"lev": lax.rem(lev + away, n_lev)},
            )
            for away in range(1, n_lev)
        ]

    def update(step, k, j):
        for low in range(0, n_i, chunk):
            r = PAD + low
            middle = field[step, k, j, pl.ds(r, chunk), :]
            spread = (
                field[step, k, j - 1, pl.ds(r, chunk), :] + field[step, k, j + 1, pl.ds(r, chunk), :]
                + field[step, k, j, pl.ds(r - 1, chunk), :] + field[step, k, j, pl.ds(r + 1, chunk), :]
                + field[step, k - 1, j, pl.ds(r, chunk), :] + field[step, k + 1, j, pl.ds(r, chunk), :]
                - 6.0 * middle
            )
            rows = pl.ds(low, chunk)
            value = middle + coeff[k - 1, j - 1, rows, :] * spread + forcing[k - 1, j - 1, rows, :]
            if step == STEPS - 1:
                last[k - 1, j - 1, rows, :] = value
                place = pl.ds(low * n_k + k - 1, chunk, stride=n_k)
                tracer_end[j - 1, place, :] = value
            else:
                field[step + 1, k, j, pl.ds(r, chunk), :] = value

    def summarise(j):
        for low in range(0, n_i, chunk):
            rows = pl.ds(low, chunk)
            total = last[0, j - 1, rows, :]
            for k in range(1, n_k):
                total = total + last[k, j - 1, rows, :]
            mean = total * (1.0 / n_k)
            squares = jnp.zeros_like(mean)
            for k in range(n_k):
                moved = last[k, j - 1, rows, :] - mean
                squares = squares + moved * moved
            own[j - 1, 0, rows, :] = mean
            own[j - 1, 1, rows, :] = squares

    def over_k(first, end, body):
        def wrapped(k, carry):
            body(k)
            return carry
        lax.fori_loop(first, end, wrapped, 0)

    for k in (0, n_k - 1):
        load(0, k, 3).start()

    barrier = pltpu.get_barrier_semaphore()

    def greet(axis, place, extent, sem):
        for away in others_near(extent):
            pl.semaphore_signal(
                sem, inc=1, device_id={axis: lax.rem(place + away, extent)}, device_id_type=MESH
            )

    greet("lat", lat, n_lat, barrier)
    greet("lon", lon, n_lon, barrier)
    for away in range(1, n_lev):
        pl.semaphore_signal(
            barrier, inc=1, device_id={"lev": lax.rem(lev + away, n_lev)}, device_id_type=MESH
        )
    expected = len(others_near(n_lat)) + len(others_near(n_lon)) + n_lev - 1
    with jax.named_scope("barrier"):
        pl.semaphore_wait(barrier, expected)
    with jax.named_scope("edges"):
        wait_for(field.at[0, pl.ds(1, 2), whole_j, inner, :], load_sem.at[3])
    for j in range(1, n_j + 1):
        send_lev(0, j)
    over_k(1, n_k - 1, lambda k: load(0, k, 0).start())
    for which in (1, 2):
        over_k(0, n_k, lambda k: load(which, k, which).start())
    for side in (0, 1):
        send_lat(0, edges, side)
    send_lon(0, edges)
    with jax.named_scope("load"):
        wait_for(field.at[0, pl.ds(1, n_k - 2), whole_j, inner, :], load_sem.at[0])
    for side in (0, 1):
        send_lat(0, middle, side)
    send_lon(0, middle)
    with jax.named_scope("load_rest"):
        wait_for(coeff, load_sem.at[1])
        wait_for(forcing, load_sem.at[2])

    def inside(step):
        with jax.named_scope(f"sides{step}"):
            wait_sides(step, middle)

        def body(k):
            def across(j, carry):
                update(step, k, j)
                return carry
            lax.fori_loop(1, n_j + 1, across, 0)

        with jax.named_scope(f"inside{step}"):
            over_k(2, n_k, body)
        if step < STEPS - 1:
            for side in (0, 1):
                send_lat(step + 1, middle, side)
            send_lon(step + 1, middle)

    def outside(step):
        with jax.named_scope(f"face_sides{step}"):
            wait_sides(step, edges)
        for j in range(1, n_j + 1):
            with jax.named_scope(f"lev{step}_{j}"):
                wait_lev(step, j)
            with jax.named_scope(f"face{step}_{j}"):
                update(step, 1, j)
                update(step, n_k, j)
            if step < STEPS - 1:
                send_lev(step + 1, j)
                for side, edge in ((0, 1), (1, n_j)):
                    if j == edge:
                        send_lat(step + 1, edges, side)
            else:
                with jax.named_scope(f"sum{j}"):
                    summarise(j)
                for copy in stat_copies(j):
                    copy.start()
        if step < STEPS - 1:
            send_lon(step + 1, edges)

    for step in range(STEPS):
        inside(step)
        outside(step)
    for j in range(1, n_j + 1):
        with jax.named_scope(f"stat{j}"):
            for copy in stat_copies(j):
                copy.wait_recv()
    with jax.named_scope("sent"):
        wait_for(field.at[:, pl.ds(0, 2), whole_j, inner, :], lev_send)
        wait_for(field.at[:, pl.ds(1, n_k), pl.ds(0, 2), inner, :], lat_send)
        wait_for(field.at[:, pl.ds(1, n_k), whole_j, pl.ds(PAD, 2), :], lon_send)
        wait_for(others, stat_send)


def finish_kernel(
    shape, n_lev, last, tracer_end, own, others, standardized_out, tracer_out, standardized, sem,
):
    n_j, n_i, n_k, _ = shape
    chunk = rows_of(n_i)

    def combine(j):
        for low in range(0, n_i, chunk):
            rows = pl.ds(low, chunk)
            means = [own[j - 1, 0, rows, :]] + [others[p, j - 1, 0, rows, :] for p in range(n_lev - 1)]
            mean = functools.reduce(jnp.add, means) * (1.0 / n_lev)
            squares = own[j - 1, 1, rows, :]
            for p in range(n_lev - 1):
                squares = squares + others[p, j - 1, 1, rows, :]
            for part in means:
                squares = squares + n_k * ((part - mean) * (part - mean))
            scale = lax.rsqrt(squares * (1.0 / (n_k * n_lev)) + EPSILON)
            for k in range(n_k):
                place = pl.ds(low * n_k + k, chunk, stride=n_k)
                standardized[j - 1, place, :] = (last[k, j - 1, rows, :] - mean) * scale

    def write(which, j):
        src, dst = ((tracer_end, tracer_out), (standardized, standardized_out))[which]
        return pltpu.make_async_copy(src.at[j], dst.at[j], sem.at[which, j])

    for j in range(n_j):
        write(0, j).start()
    for j in range(n_j):
        combine(j + 1)
        write(1, j).start()
    for which in (0, 1):
        for j in range(n_j):
            write(which, j).wait()


def on_device(sizes, tracer, diffusivity, source):
    shape = tracer.shape
    n_j, n_i, n_k, levels = shape
    n_lev = sizes[2]
    f32 = jnp.float32
    sem = pltpu.SemaphoreType.DMA
    flat = (n_j, n_i * n_k, levels)
    parts = (
        pltpu.VMEM((n_k, n_j, n_i, levels), f32),
        pltpu.VMEM(flat, f32),
        pltpu.VMEM((n_j, 2, n_i, levels), f32),
        pltpu.VMEM((n_lev - 1, n_j, 2, n_i, levels), f32),
    )
    results = pl.pallas_call(
        functools.partial(steps_kernel, sizes, shape),
        out_shape=parts,
        in_specs=[pl.BlockSpec(memory_space=pl.ANY)] * 3,
        out_specs=(pl.BlockSpec(memory_space=pltpu.VMEM),) * len(parts),
        scratch_shapes=[
            pltpu.VMEM((STEPS, n_k + 2, n_j + 2, n_i + 2 * PAD, levels), f32),
            pltpu.VMEM((n_k, n_j, n_i, levels), f32),
            pltpu.VMEM((n_k, n_j, n_i, levels), f32),
            sem((4,)),
            sem, sem((2, n_j)),
            sem, sem((2, 2)),
            sem, sem((2, 2)),
            sem, sem((n_lev - 1, n_j)),
        ],
        compiler_params=pltpu.CompilerParams(
            collective_id=0, has_side_effects=True, vmem_limit_bytes=48 * 1024 * 1024,
        ),
    )(tracer, diffusivity, source)
    standardized, tracer_end = pl.pallas_call(
        functools.partial(finish_kernel, shape, n_lev),
        out_shape=(jax.ShapeDtypeStruct(flat, f32),) * 2,
        in_specs=[pl.BlockSpec(memory_space=pltpu.VMEM)] * len(parts),
        out_specs=(pl.BlockSpec(memory_space=pl.ANY),) * 2,
        scratch_shapes=[pltpu.VMEM(flat, f32), sem((2, n_j))],
        compiler_params=pltpu.CompilerParams(vmem_limit_bytes=8 * 1024 * 1024),
    )(*results)
    return standardized.reshape(shape), tracer_end.reshape(shape)


def solution(mesh):
    sizes = (mesh.shape["lat"], mesh.shape["lon"], mesh.shape["lev"])
    spec = P(("unit", "lat"), "lon", "lev", None)
    return jax.shard_map(
        functools.partial(on_device, sizes),
        mesh=mesh,
        in_specs=(spec, spec, spec),
        out_specs=(spec, spec),
        check_vma=False,
    )
```

time: 67.8 us -> 65.5 us (0.966)
  Pallas kernels: 67 us -> 64.7 us
    pallas_call x2, Pallas kernels: 67 us -> 64.7 us  [the longest x1 61.4 us: on_device(): pl.pallas_call(functools.partial(steps_kernel, sizes, shape), out_shape=p...]
where the time goes in v2:
time: 65.5 us; the launch traced here: 65.4 us
  Pallas kernels  64.7 us (99%)
    pallas_call x1, Pallas kernels, on_device(): pl.pallas_call(functools.partial(steps_kernel, sizes, shape), out_shape=p...  61.4 us
    pallas_call x1, Pallas kernels, on_device(): pl.pallas_call(functools.partial(finish_kernel, shape, n_lev), out_shape=...  3.37 us

profile of v2, /device:TPU:0, one launch (start us, length us, event | category | flops | bytes accessed | tf_op | source)
XLA Modules:
  0.0 65.4 jit_solution(16267590666889222788)
XLA Ops:
  0.6 61.4 %shard_map.50 = (f32[16,4,128,128]{3,2,1,0:T(8,128)S(1)}, f32[4,2048,128]{2,1,0:T(8,128)S(1)}, f32[4,2,128,128]{3,2,1,0:T(8,128)S(1)}, f32[1,4,2,128,128]{4,3,2,1,0:T(8,128)S(1)}) custom-call(f32[4,128,16,128]{3,2,1,0:T(8,128)} %tracer.1, f32[4,128,16,128]{3,2,1,0:T(8,128)} %diffusivity.1, f32[4,128,16,128]{3,2,1,0:T(8,128)} %source.1), custom_call_target="tpu_custom_call" | custom-call | tf_op jit(solution)/shard_map/pallas_call | solution.py:286
  62.0 3.4 %shard_map.51 = (f32[4,2048,128]{2,1,0:T(8,128)}, f32[4,2048,128]{2,1,0:T(8,128)}) custom-call(f32[16,4,128,128]{3,2,1,0:T(8,128)S(1)} %get-tuple-element.8.last, f32[4,2048,128]{2,1,0:T(8,128)S(1)} %get-tuple-element.9.tracer_end, f32[4,2,128,128]{3,2,1,0:T(8,128)S(1)} %get-tuple-element.10.own, f32[1,4,2,128,128]{4,3,2,1,0:T(8,128)S(1)} %get-tuple-element.11.others), custom_call_target="tpu_custom_call" | custom-call | tf_op jit(solution)/shard_map/pallas_call | solution.py:305

commit v3 on v2

--- a/solution.py
+++ b/solution.py
@@ -27,7 +27,7 @@
 def steps_kernel(
     sizes, shape, tracer, diffusivity, source, last, tracer_end, own, others,
     field, coeff, forcing,
-    load_sem, lev_send, lev_recv, lat_send, lat_recv, lon_send, lon_recv, stat_send, stat_recv,
+    load_sem, lev_send, lev_recv, lat_send, lat_recv, lon_send, lon_recv, stat_send, stat_recv, ready,
 ):
     n_j, n_i, n_k, _ = shape
     n_lat, n_lon, n_lev = sizes
@@ -46,6 +46,11 @@
         else:
             target = (coeff, forcing)[which - 1].at[k]
         return pltpu.make_async_copy(array.at[:, :, k, :], target, load_sem.at[sem])
+
+    def load_edge(j, k):
+        return pltpu.make_async_copy(
+            tracer.at[j - 1, :, k, :], field.at[0, k + 1, j, inner, :], load_sem.at[2 + j]
+        )
 
     def wait_for(ref, sem):
         pltpu.make_async_copy(ref, ref, sem).wait()
@@ -143,8 +148,9 @@
             return carry
         lax.fori_loop(first, end, wrapped, 0)
 
-    for k in (0, n_k - 1):
-        load(0, k, 3).start()
+    for j in range(1, n_j + 1):
+        for k in (0, n_k - 1):
+            load_edge(j, k).start()
 
     barrier = pltpu.get_barrier_semaphore()
 
@@ -154,22 +160,38 @@
                 sem, inc=1, device_id={axis: lax.rem(place + away, extent)}, device_id_type=MESH
             )
 
-    greet("lat", lat, n_lat, barrier)
-    greet("lon", lon, n_lon, barrier)
+    sides = (("lat", lat, n_lat), ("lon", lon, n_lon))
+    pairs = [extent % 2 == 0 for _, _, extent in sides]
+    expected = n_lev - 1
     for away in range(1, n_lev):
         pl.semaphore_signal(
             barrier, inc=1, device_id={"lev": lax.rem(lev + away, n_lev)}, device_id_type=MESH
         )
-    expected = len(others_near(n_lat)) + len(others_near(n_lon)) + n_lev - 1
+    for paired, (axis, place, extent) in zip(pairs, sides):
+        if paired:
+            pl.when(lax.rem(place, 2) == 0)(functools.partial(greet, axis, place, extent, barrier))
+            expected = expected + lax.rem(place, 2) * len(others_near(extent))
+        else:
+            greet(axis, place, extent, barrier)
+            expected = expected + len(others_near(extent))
     with jax.named_scope("barrier"):
         pl.semaphore_wait(barrier, expected)
-    with jax.named_scope("edges"):
-        wait_for(field.at[0, pl.ds(1, 2), whole_j, inner, :], load_sem.at[3])
     for j in range(1, n_j + 1):
+        wait_for(field.at[0, pl.ds(1, 2), j, inner, :], load_sem.at[2 + j])
         send_lev(0, j)
     over_k(1, n_k - 1, lambda k: load(0, k, 0).start())
     for which in (1, 2):
         over_k(0, n_k, lambda k: load(which, k, which).start())
+    for n, (paired, (axis, place, extent)) in enumerate(zip(pairs, sides)):
+        if paired:
+            @pl.when(lax.rem(place, 2) == 1)
+            def _():
+                greet(axis, place, extent, ready.at[n])
+
+            @pl.when(lax.rem(place, 2) == 0)
+            def _():
+                pl.semaphore_wait(ready.at[n], len(others_near(extent)))
+
     for side in (0, 1):
         send_lat(0, edges, side)
     send_lon(0, edges)
@@ -292,11 +314,12 @@
             pltpu.VMEM((STEPS, n_k + 2, n_j + 2, n_i + 2 * PAD, levels), f32),
             pltpu.VMEM((n_k, n_j, n_i, levels), f32),
             pltpu.VMEM((n_k, n_j, n_i, levels), f32),
-            sem((4,)),
+            sem((n_j + 3,)),
             sem, sem((2, n_j)),
             sem, sem((2, 2)),
             sem, sem((2, 2)),
             sem, sem((n_lev - 1, n_j)),
+            pltpu.SemaphoreType.REGULAR((2,)),
         ],
         compiler_params=pltpu.CompilerParams(
             collective_id=0, has_side_effects=True, vmem_limit_bytes=48 * 1024 * 1024,

time: 65.5 us -> 65.2 us (level)
  no operation moved by 1% of the time
where the time goes in v3:
time: 65.2 us; the launch traced here: 65 us
  Pallas kernels  64.4 us (99%)
    pallas_call x1, Pallas kernels, on_device(): pl.pallas_call(functools.partial(steps_kernel, sizes, shape), out_shape=p...  61 us
    pallas_call x1, Pallas kernels, on_device(): pl.pallas_call(functools.partial(finish_kernel, shape, n_lev), out_shape=...  3.37 us

profile of v3, /device:TPU:0, one launch (start us, length us, event | category | flops | bytes accessed | tf_op | source)
XLA Modules:
  0.0 65.0 jit_solution(14033815501585537792)
XLA Ops:
  0.6 61.0 %shard_map.50 = (f32[16,4,128,128]{3,2,1,0:T(8,128)S(1)}, f32[4,2048,128]{2,1,0:T(8,128)S(1)}, f32[4,2,128,128]{3,2,1,0:T(8,128)S(1)}, f32[1,4,2,128,128]{4,3,2,1,0:T(8,128)S(1)}) custom-call(f32[4,128,16,128]{3,2,1,0:T(8,128)} %tracer.1, f32[4,128,16,128]{3,2,1,0:T(8,128)} %diffusivity.1, f32[4,128,16,128]{3,2,1,0:T(8,128)} %source.1), custom_call_target="tpu_custom_call" | custom-call | tf_op jit(solution)/shard_map/pallas_call | solution.py:308
  61.7 3.4 %shard_map.51 = (f32[4,2048,128]{2,1,0:T(8,128)}, f32[4,2048,128]{2,1,0:T(8,128)}) custom-call(f32[16,4,128,128]{3,2,1,0:T(8,128)S(1)} %get-tuple-element.8.last, f32[4,2048,128]{2,1,0:T(8,128)S(1)} %get-tuple-element.9.tracer_end, f32[4,2,128,128]{3,2,1,0:T(8,128)S(1)} %get-tuple-element.10.own, f32[1,4,2,128,128]{4,3,2,1,0:T(8,128)S(1)} %get-tuple-element.11.others), custom_call_target="tpu_custom_call" | custom-call | tf_op jit(solution)/shard_map/pallas_call | solution.py:328

commit v4 on v3

--- a/solution.py
+++ b/solution.py
@@ -38,6 +38,8 @@
     lat_up, lat_down = lax.rem(lat + 1, n_lat), lax.rem(lat + n_lat - 1, n_lat)
     lon_up, lon_down = lax.rem(lon + 1, n_lon), lax.rem(lon + n_lon - 1, n_lon)
     lev_up, lev_down = lax.rem(lev + 1, n_lev), lax.rem(lev + n_lev - 1, n_lev)
+
+    first_half = lax.rem(lat, 2) == 0
 
     def load(which, k, sem):
         array = (tracer, diffusivity, source)[which]
@@ -238,58 +240,123 @@
             else:
                 with jax.named_scope(f"sum{j}"):
                     summarise(j)
-                for copy in stat_copies(j):
-                    copy.start()
+                @pl.when(first_half)
+                def _():
+                    for copy in stat_copies(j):
+                        copy.start()
         if step < STEPS - 1:
             send_lon(step + 1, edges)
 
     for step in range(STEPS):
         inside(step)
         outside(step)
-    for j in range(1, n_j + 1):
-        with jax.named_scope(f"stat{j}"):
-            for copy in stat_copies(j):
-                copy.wait_recv()
+
+    @pl.when(first_half)
+    def _():
+        for j in range(1, n_j + 1):
+            with jax.named_scope(f"stat{j}"):
+                for copy in stat_copies(j):
+                    copy.wait_recv()
+        wait_for(others, stat_send)
+
     with jax.named_scope("sent"):
         wait_for(field.at[:, pl.ds(0, 2), whole_j, inner, :], lev_send)
         wait_for(field.at[:, pl.ds(1, n_k), pl.ds(0, 2), inner, :], lat_send)
         wait_for(field.at[:, pl.ds(1, n_k), whole_j, pl.ds(PAD, 2), :], lon_send)
-        wait_for(others, stat_send)
-
-
-def finish_kernel(
-    shape, n_lev, last, tracer_end, own, others, standardized_out, tracer_out, standardized, sem,
-):
+
+
+def combine(shape, n_lev, j, last, own, others, place_of):
     n_j, n_i, n_k, _ = shape
     chunk = rows_of(n_i)
-
-    def combine(j):
-        for low in range(0, n_i, chunk):
-            rows = pl.ds(low, chunk)
-            means = [own[j - 1, 0, rows, :]] + [others[p, j - 1, 0, rows, :] for p in range(n_lev - 1)]
-            mean = functools.reduce(jnp.add, means) * (1.0 / n_lev)
-            squares = own[j - 1, 1, rows, :]
-            for p in range(n_lev - 1):
-                squares = squares + others[p, j - 1, 1, rows, :]
-            for part in means:
-                squares = squares + n_k * ((part - mean) * (part - mean))
-            scale = lax.rsqrt(squares * (1.0 / (n_k * n_lev)) + EPSILON)
-            for k in range(n_k):
-                place = pl.ds(low * n_k + k, chunk, stride=n_k)
-                standardized[j - 1, place, :] = (last[k, j - 1, rows, :] - mean) * scale
-
-    def write(which, j):
-        src, dst = ((tracer_end, tracer_out), (standardized, standardized_out))[which]
-        return pltpu.make_async_copy(src.at[j], dst.at[j], sem.at[which, j])
+    for low in range(0, n_i, chunk):
+        rows = pl.ds(low, chunk)
+        means = [own[j, 0, rows, :]] + [others[p, j, 0, rows, :] for p in range(n_lev - 1)]
+        mean = functools.reduce(jnp.add, means) * (1.0 / n_lev)
+        squares = own[j, 1, rows, :]
+        for p in range(n_lev - 1):
+            squares = squares + others[p, j, 1, rows, :]
+        for part in means:
+            squares = squares + n_k * ((part - mean) * (part - mean))
+        scale = lax.rsqrt(squares * (1.0 / (n_k * n_lev)) + EPSILON)
+        for k in range(n_k):
+            place = pl.ds(low * n_k + k, chunk, stride=n_k)
+            place_of[place, :] = (last[k, j, rows, :] - mean) * scale
+
+
+def write_tracer(tracer_end, out, token, sem):
+    copies = [
+        pltpu.make_async_copy(tracer_end.at[j], out.at[j], sem.at[j])
+        for j in range(tracer_end.shape[0])
+    ]
+    for copy in copies:
+        copy.start()
+    token[...] = jnp.zeros_like(token)
+    for copy in copies:
+        copy.wait()
+
+
+def second_kernel(
+    sizes, shape, last, own, early, token, others, standardized, send_sem, recv_sem,
+):
+    n_j, n_i, _, _ = shape
+    n_lev = sizes[2]
+    lat, lev = lax.axis_index("lat"), lax.axis_index("lev")
+    second_half = lax.rem(lat, 2) == 1
+
+    def copies(j):
+        return [
+            pltpu.make_async_remote_copy(
+                src_ref=own.at[j], dst_ref=others.at[n_lev - 1 - away, j],
+                send_sem=send_sem, recv_sem=recv_sem.at[n_lev - 1 - away, j],
+                device_id={"lev": lax.rem(lev + away, n_lev)}, device_id_type=MESH,
+            )
+            for away in range(1, n_lev)
+        ]
+
+    @pl.when(second_half)
+    def _():
+        barrier = pltpu.get_barrier_semaphore()
+        for away in range(1, n_lev):
+            pl.semaphore_signal(
+                barrier, inc=1, device_id={"lev": lax.rem(lev + away, n_lev)}, device_id_type=MESH
+            )
+        with jax.named_scope("barrier2"):
+            pl.semaphore_wait(barrier, n_lev - 1)
+        for j in range(n_j):
+            for copy in copies(j):
+                copy.start()
+
+    @pl.when(lax.rem(lat, 2) == 0)
+    def _():
+        others[...] = early[...]
 
     for j in range(n_j):
-        write(0, j).start()
-    for j in range(n_j):
-        combine(j + 1)
-        write(1, j).start()
-    for which in (0, 1):
-        for j in range(n_j):
-            write(which, j).wait()
+        @pl.when(second_half)
+        def _():
+            with jax.named_scope(f"late{j}"):
+                for copy in copies(j):
+                    copy.wait_recv()
+
+        if j < n_j - 1:
+            combine(shape, n_lev, j, last, own, others, standardized.at[j])
+
+    @pl.when(second_half)
+    def _():
+        pltpu.make_async_copy(others, others, send_sem).wait()
+
+
+def finish_kernel(shape, n_lev, last, own, others, ready, out, final, sem):
+    n_j = shape[0]
+    copies = [
+        pltpu.make_async_copy(final if j == n_j - 1 else ready.at[j], out.at[j], sem.at[j])
+        for j in range(n_j)
+    ]
+    for copy in copies[:-1]:
+        copy.start()
+    combine(shape, n_lev, n_j - 1, last, own, others, final)
+    copies[-1].start()
+    for copy in copies:
+        copy.wait()
 
 
 def on_device(sizes, tracer, diffusivity, source):
@@ -305,7 +372,7 @@
         pltpu.VMEM((n_j, 2, n_i, levels), f32),
         pltpu.VMEM((n_lev - 1, n_j, 2, n_i, levels), f32),
     )
-    results = pl.pallas_call(
+    last, tracer_end, own, early = pl.pallas_call(
         functools.partial(steps_kernel, sizes, shape),
         out_shape=parts,
         in_specs=[pl.BlockSpec(memory_space=pl.ANY)] * 3,
@@ -325,14 +392,33 @@
             collective_id=0, has_side_effects=True, vmem_limit_bytes=48 * 1024 * 1024,
         ),
     )(tracer, diffusivity, source)
-    standardized, tracer_end = pl.pallas_call(
+    in_vmem, in_hbm = pl.BlockSpec(memory_space=pltpu.VMEM), pl.BlockSpec(memory_space=pl.ANY)
+    tracer_end, token = pl.pallas_call(
+        write_tracer,
+        out_shape=(jax.ShapeDtypeStruct(flat, f32), pltpu.VMEM((8, levels), f32)),
+        in_specs=[in_vmem],
+        out_specs=(in_hbm, in_vmem),
+        scratch_shapes=[sem((n_j,))],
+        compiler_params=pltpu.CompilerParams(vmem_limit_bytes=1024 * 1024),
+    )(tracer_end)
+    others, standardized = pl.pallas_call(
+        functools.partial(second_kernel, sizes, shape),
+        out_shape=(parts[3], pltpu.VMEM(flat, f32)),
+        in_specs=[in_vmem] * 4,
+        out_specs=(in_vmem,) * 2,
+        scratch_shapes=[sem, sem((n_lev - 1, n_j))],
+        compiler_params=pltpu.CompilerParams(
+            collective_id=1, has_side_effects=True, vmem_limit_bytes=8 * 1024 * 1024,
+        ),
+    )(last, own, early, token)
+    standardized = pl.pallas_call(
         functools.partial(finish_kernel, shape, n_lev),
-        out_shape=(jax.ShapeDtypeStruct(flat, f32),) * 2,
-        in_specs=[pl.BlockSpec(memory_space=pltpu.VMEM)] * len(parts),
-        out_specs=(pl.BlockSpec(memory_space=pl.ANY),) * 2,
-        scratch_shapes=[pltpu.VMEM(flat, f32), sem((2, n_j))],
-        compiler_params=pltpu.CompilerParams(vmem_limit_bytes=8 * 1024 * 1024),
-    )(*results)
+        out_shape=jax.ShapeDtypeStruct(flat, f32),
+        in_specs=[in_vmem] * 4,
+        out_specs=in_hbm,
+        scratch_shapes=[pltpu.VMEM(flat[1:], f32), sem((n_j,))],
+        compiler_params=pltpu.CompilerParams(vmem_limit_bytes=4 * 1024 * 1024),
+    )(last, own, others, standardized)
     return standardized.reshape(shape), tracer_end.reshape(shape)
 
 

time: 65.2 us -> 62.9 us (0.965)
  Pallas kernels: 64.4 us -> 62 us
    pallas_call x1, Pallas kernels: 61 us -> 56.5 us  [on_device(): pl.pallas_call(functools.partial(steps_kernel, sizes, shape), out_shape=p...]
    pallas_call x0 -> x2, Pallas kernels: none -> 3.44 us  [the longest x1 2.04 us: on_device(): pl.pallas_call(write_tracer, out_shape=(jax.ShapeDtypeStruct(flat, f32),...]
    pallas_call x1, Pallas kernels: 3.37 us -> 2.04 us  [on_device(): pl.pallas_call(functools.partial(finish_kernel, shape, n_lev), out_shape=...]
where the time goes in v4:
time: 62.9 us; the launch traced here: 62.6 us
  Pallas kernels  62 us (99%)
  between operations  0.65 us (1%)
    pallas_call x1, Pallas kernels, on_device(): pl.pallas_call(functools.partial(steps_kernel, sizes, shape), out_shape=p...  56.5 us
    pallas_call x1, Pallas kernels, on_device(): pl.pallas_call(write_tracer, out_shape=(jax.ShapeDtypeStruct(flat, f32),...  2.04 us
    pallas_call x1, Pallas kernels, on_device(): pl.pallas_call(functools.partial(finish_kernel, shape, n_lev), out_shape=...  2.04 us
    pallas_call x1, Pallas kernels, on_device(): pl.pallas_call(functools.partial(second_kernel, sizes, shape), out_shape=...  1.39 us

profile of v4, /device:TPU:0, one launch (start us, length us, event | category | flops | bytes accessed | tf_op | source)
XLA Modules:
  0.0 62.6 jit_solution(5532686393925229036)
XLA Ops:
  0.6 56.5 %shard_map.50 = (f32[16,4,128,128]{3,2,1,0:T(8,128)S(1)}, f32[4,2048,128]{2,1,0:T(8,128)S(1)}, f32[4,2,128,128]{3,2,1,0:T(8,128)S(1)}, f32[1,4,2,128,128]{4,3,2,1,0:T(8,128)S(1)}) custom-call(f32[4,128,16,128]{3,2,1,0:T(8,128)} %tracer.1, f32[4,128,16,128]{3,2,1,0:T(8,128)} %diffusivity.1, f32[4,128,16,128]{3,2,1,0:T(8,128)} %source.1), custom_call_target="tpu_custom_call" | custom-call | tf_op jit(solution)/shard_map/pallas_call | solution.py:375
  57.1 2.0 %shard_map.51 = (f32[4,2048,128]{2,1,0:T(8,128)}, f32[8,128]{1,0:T(8,128)S(1)}) custom-call(f32[4,2048,128]{2,1,0:T(8,128)S(1)} %get-tuple-element.13.tracer_end), custom_call_target="tpu_custom_call" | custom-call | tf_op jit(solution)/shard_map/pallas_call | solution.py:396
  59.2 1.4 %shard_map.52 = (f32[1,4,2,128,128]{4,3,2,1,0:T(8,128)S(1)}, f32[4,2048,128]{2,1,0:T(8,128)S(1)}) custom-call(f32[16,4,128,128]{3,2,1,0:T(8,128)S(1)} %get-tuple-element.10.last, f32[4,2,128,128]{3,2,1,0:T(8,128)S(1)} %get-tuple-element.11.own, f32[1,4,2,128,128]{4,3,2,1,0:T(8,128)S(1)} %get-tuple-element.12.early, f32[8,128]{1,0:T(8,128)S(1)} %get-tuple-element.14.token), custom_call_target="tpu_custom_call" | custom-call | tf_op jit(solution)/shard_map/pallas_call | solution.py:404
  60.6 2.0 %shard_map.53 = f32[4,2048,128]{2,1,0:T(8,128)} custom-call(f32[16,4,128,128]{3,2,1,0:T(8,128)S(1)} %get-tuple-element.10.last, f32[4,2,128,128]{3,2,1,0:T(8,128)S(1)} %get-tuple-element.11.own, f32[1,4,2,128,128]{4,3,2,1,0:T(8,128)S(1)} %get-tuple-element.15.others, f32[4,2048,128]{2,1,0:T(8,128)S(1)} %get-tuple-element.16.ready), custom_call_target="tpu_custom_call" | custom-call | tf_op jit(solution)/shard_map/pallas_call | solution.py:414

commit v5 on v4

--- a/solution.py
+++ b/solution.py
@@ -49,9 +49,19 @@
             target = (coeff, forcing)[which - 1].at[k]
         return pltpu.make_async_copy(array.at[:, :, k, :], target, load_sem.at[sem])
 
-    def load_edge(j, k):
+    first = chunk if n_i > chunk else n_i
+
+    def pieces(j):
+        if j > 1 or first == n_i:
+            return ((0, n_i),)
+        return ((0, first), (first, n_i - first))
+
+    def load_edge(j, k, piece):
+        low, size = piece
+        sem = 3 + n_j if (j == 1 and low > 0) else 2 + j
         return pltpu.make_async_copy(
-            tracer.at[j - 1, :, k, :], field.at[0, k + 1, j, inner, :], load_sem.at[2 + j]
+            tracer.at[j - 1, pl.ds(low, size), k, :],
+            field.at[0, k + 1, j, pl.ds(PAD + low, size), :], load_sem.at[sem],
         )
 
     def wait_for(ref, sem):
@@ -63,11 +73,13 @@
             device_id=device, device_id_type=MESH,
         )
 
-    def send_lev(step, j):
+    def send_lev(step, j, piece=None):
+        low, size = piece or (0, n_i)
+        rows = pl.ds(PAD + low, size)
         recv = lev_recv.at[step % 2, j - 1]
         for edge, halo, to in ((1, n_k + 1, lev_down), (n_k, 0, lev_up)):
-            src = field.at[step, edge, j, inner, :]
-            remote(src, field.at[step, halo, j, inner, :], lev_send, recv, {"lev": to}).start()
+            src = field.at[step, edge, j, rows, :]
+            remote(src, field.at[step, halo, j, rows, :], lev_send, recv, {"lev": to}).start()
 
     def wait_lev(step, j):
         wait_for(field.at[step, pl.ds(0, 2), j, inner, :], lev_recv.at[step % 2, j - 1])
@@ -151,8 +163,9 @@
         lax.fori_loop(first, end, wrapped, 0)
 
     for j in range(1, n_j + 1):
-        for k in (0, n_k - 1):
-            load_edge(j, k).start()
+        for piece in pieces(j):
+            for k in (0, n_k - 1):
+                load_edge(j, k, piece).start()
 
     barrier = pltpu.get_barrier_semaphore()
 
@@ -179,8 +192,11 @@
     with jax.named_scope("barrier"):
         pl.semaphore_wait(barrier, expected)
     for j in range(1, n_j + 1):
-        wait_for(field.at[0, pl.ds(1, 2), j, inner, :], load_sem.at[2 + j])
-        send_lev(0, j)
+        for piece in pieces(j):
+            low, size = piece
+            sem = 3 + n_j if (j == 1 and low > 0) else 2 + j
+            wait_for(field.at[0, pl.ds(1, 2), j, pl.ds(PAD + low, size), :], load_sem.at[sem])
+            send_lev(0, j, piece)
     over_k(1, n_k - 1, lambda k: load(0, k, 0).start())
     for which in (1, 2):
         over_k(0, n_k, lambda k: load(which, k, which).start())
@@ -284,15 +300,10 @@
 
 
 def write_tracer(tracer_end, out, token, sem):
-    copies = [
-        pltpu.make_async_copy(tracer_end.at[j], out.at[j], sem.at[j])
-        for j in range(tracer_end.shape[0])
-    ]
-    for copy in copies:
-        copy.start()
+    copy = pltpu.make_async_copy(tracer_end, out, sem)
+    copy.start()
     token[...] = jnp.zeros_like(token)
-    for copy in copies:
-        copy.wait()
+    copy.wait()
 
 
 def second_kernel(
@@ -347,16 +358,14 @@
 
 def finish_kernel(shape, n_lev, last, own, others, ready, out, final, sem):
     n_j = shape[0]
-    copies = [
-        pltpu.make_async_copy(final if j == n_j - 1 else ready.at[j], out.at[j], sem.at[j])
-        for j in range(n_j)
-    ]
-    for copy in copies[:-1]:
-        copy.start()
+    most = pl.ds(0, n_j - 1)
+    earlier = pltpu.make_async_copy(ready.at[most], out.at[most], sem.at[0])
+    latest = pltpu.make_async_copy(final, out.at[n_j - 1], sem.at[1])
+    earlier.start()
     combine(shape, n_lev, n_j - 1, last, own, others, final)
-    copies[-1].start()
-    for copy in copies:
-        copy.wait()
+    latest.start()
+    earlier.wait()
+    latest.wait()
 
 
 def on_device(sizes, tracer, diffusivity, source):
@@ -381,7 +390,7 @@
             pltpu.VMEM((STEPS, n_k + 2, n_j + 2, n_i + 2 * PAD, levels), f32),
             pltpu.VMEM((n_k, n_j, n_i, levels), f32),
             pltpu.VMEM((n_k, n_j, n_i, levels), f32),
-            sem((n_j + 3,)),
+            sem((n_j + 4,)),
             sem, sem((2, n_j)),
             sem, sem((2, 2)),
             sem, sem((2, 2)),
@@ -398,7 +407,7 @@
         out_shape=(jax.ShapeDtypeStruct(flat, f32), pltpu.VMEM((8, levels), f32)),
         in_specs=[in_vmem],
         out_specs=(in_hbm, in_vmem),
-        scratch_shapes=[sem((n_j,))],
+        scratch_shapes=[sem],
         compiler_params=pltpu.CompilerParams(vmem_limit_bytes=1024 * 1024),
     )(tracer_end)
     others, standardized = pl.pallas_call(
@@ -416,7 +425,7 @@
         out_shape=jax.ShapeDtypeStruct(flat, f32),
         in_specs=[in_vmem] * 4,
         out_specs=in_hbm,
-        scratch_shapes=[pltpu.VMEM(flat[1:], f32), sem((n_j,))],
+        scratch_shapes=[pltpu.VMEM(flat[1:], f32), sem((2,))],
         compiler_params=pltpu.CompilerParams(vmem_limit_bytes=4 * 1024 * 1024),
     )(last, own, others, standardized)
     return standardized.reshape(shape), tracer_end.reshape(shape)

time: 62.9 us -> 62.8 us (level)
  no operation moved by 1% of the time
where the time goes in v5:
time: 62.8 us; the launch traced here: 62.5 us
  Pallas kernels  61.8 us (98%)
  between operations  0.65 us (1%)
    pallas_call x1, Pallas kernels, on_device(): pl.pallas_call(functools.partial(steps_kernel, sizes, shape), out_shape=p...  56.4 us
    pallas_call x1, Pallas kernels, on_device(): pl.pallas_call(functools.partial(finish_kernel, shape, n_lev), out_shape=...  2.02 us
    pallas_call x1, Pallas kernels, on_device(): pl.pallas_call(write_tracer, out_shape=(jax.ShapeDtypeStruct(flat, f32),...  2.02 us
    pallas_call x1, Pallas kernels, on_device(): pl.pallas_call(functools.partial(second_kernel, sizes, shape), out_shape=...  1.39 us

profile of v5, /device:TPU:0, one launch (start us, length us, event | category | flops | bytes accessed | tf_op | source)
XLA Modules:
  0.0 62.5 jit_solution(4514654370330905885)
XLA Ops:
  0.6 56.4 %shard_map.50 = (f32[16,4,128,128]{3,2,1,0:T(8,128)S(1)}, f32[4,2048,128]{2,1,0:T(8,128)S(1)}, f32[4,2,128,128]{3,2,1,0:T(8,128)S(1)}, f32[1,4,2,128,128]{4,3,2,1,0:T(8,128)S(1)}) custom-call(f32[4,128,16,128]{3,2,1,0:T(8,128)} %tracer.1, f32[4,128,16,128]{3,2,1,0:T(8,128)} %diffusivity.1, f32[4,128,16,128]{3,2,1,0:T(8,128)} %source.1), custom_call_target="tpu_custom_call" | custom-call | tf_op jit(solution)/shard_map/pallas_call | solution.py:384
  57.0 2.0 %shard_map.51 = (f32[4,2048,128]{2,1,0:T(8,128)}, f32[8,128]{1,0:T(8,128)S(1)}) custom-call(f32[4,2048,128]{2,1,0:T(8,128)S(1)} %get-tuple-element.13.tracer_end), custom_call_target="tpu_custom_call" | custom-call | tf_op jit(solution)/shard_map/pallas_call | solution.py:405
  59.0 1.4 %shard_map.52 = (f32[1,4,2,128,128]{4,3,2,1,0:T(8,128)S(1)}, f32[4,2048,128]{2,1,0:T(8,128)S(1)}) custom-call(f32[16,4,128,128]{3,2,1,0:T(8,128)S(1)} %get-tuple-element.10.last, f32[4,2,128,128]{3,2,1,0:T(8,128)S(1)} %get-tuple-element.11.own, f32[1,4,2,128,128]{4,3,2,1,0:T(8,128)S(1)} %get-tuple-element.12.early, f32[8,128]{1,0:T(8,128)S(1)} %get-tuple-element.14.token), custom_call_target="tpu_custom_call" | custom-call | tf_op jit(solution)/shard_map/pallas_call | solution.py:413
  60.4 2.0 %shard_map.53 = f32[4,2048,128]{2,1,0:T(8,128)} custom-call(f32[16,4,128,128]{3,2,1,0:T(8,128)S(1)} %get-tuple-element.10.last, f32[4,2,128,128]{3,2,1,0:T(8,128)S(1)} %get-tuple-element.11.own, f32[1,4,2,128,128]{4,3,2,1,0:T(8,128)S(1)} %get-tuple-element.15.others, f32[4,2048,128]{2,1,0:T(8,128)S(1)} %get-tuple-element.16.ready), custom_call_target="tpu_custom_call" | custom-call | tf_op jit(solution)/shard_map/pallas_call | solution.py:423

commit v6 on v5

--- a/solution.py
+++ b/solution.py
@@ -172,10 +172,11 @@
     def greet(axis, place, extent, sem):
         for away in others_near(extent):
             pl.semaphore_signal(
-                sem, inc=1, device_id={axis: lax.rem(place + away, extent)}, device_id_type=MESH
+                sem, inc=1, device_id={axis: lax.rem(lax.axis_index(axis) + away, extent)},
+                device_id_type=MESH,
             )
 
-    sides = (("lat", lat, n_lat), ("lon", lon, n_lon))
+    sides = (("lat", lat + 1, n_lat), ("lon", lon, n_lon))
     pairs = [extent % 2 == 0 for _, _, extent in sides]
     expected = n_lev - 1
     for away in range(1, n_lev):

time: 62.8 us -> 62.8 us (level)
  no operation moved by 1% of the time
where the time goes in v6:
time: 62.8 us; the launch traced here: 62.5 us
  Pallas kernels  61.8 us (98%)
  between operations  0.65 us (1%)
    pallas_call x1, Pallas kernels, on_device(): pl.pallas_call(functools.partial(steps_kernel, sizes, shape), out_shape=p...  56.4 us
    pallas_call x1, Pallas kernels, on_device(): pl.pallas_call(functools.partial(finish_kernel, shape, n_lev), out_shape=...  2.02 us
    pallas_call x1, Pallas kernels, on_device(): pl.pallas_call(write_tracer, out_shape=(jax.ShapeDtypeStruct(flat, f32),...  2.02 us
    pallas_call x1, Pallas kernels, on_device(): pl.pallas_call(functools.partial(second_kernel, sizes, shape), out_shape=...  1.39 us

profile of v6, /device:TPU:0, one launch (start us, length us, event | category | flops | bytes accessed | tf_op | source)
XLA Modules:
  0.0 62.5 jit_solution(6990043738507489807)
XLA Ops:
  0.6 56.4 %shard_map.50 = (f32[16,4,128,128]{3,2,1,0:T(8,128)S(1)}, f32[4,2048,128]{2,1,0:T(8,128)S(1)}, f32[4,2,128,128]{3,2,1,0:T(8,128)S(1)}, f32[1,4,2,128,128]{4,3,2,1,0:T(8,128)S(1)}) custom-call(f32[4,128,16,128]{3,2,1,0:T(8,128)} %tracer.1, f32[4,128,16,128]{3,2,1,0:T(8,128)} %diffusivity.1, f32[4,128,16,128]{3,2,1,0:T(8,128)} %source.1), custom_call_target="tpu_custom_call" | custom-call | tf_op jit(solution)/shard_map/pallas_call | solution.py:385
  57.0 2.0 %shard_map.51 = (f32[4,2048,128]{2,1,0:T(8,128)}, f32[8,128]{1,0:T(8,128)S(1)}) custom-call(f32[4,2048,128]{2,1,0:T(8,128)S(1)} %get-tuple-element.13.tracer_end), custom_call_target="tpu_custom_call" | custom-call | tf_op jit(solution)/shard_map/pallas_call | solution.py:406
  59.0 1.4 %shard_map.52 = (f32[1,4,2,128,128]{4,3,2,1,0:T(8,128)S(1)}, f32[4,2048,128]{2,1,0:T(8,128)S(1)}) custom-call(f32[16,4,128,128]{3,2,1,0:T(8,128)S(1)} %get-tuple-element.10.last, f32[4,2,128,128]{3,2,1,0:T(8,128)S(1)} %get-tuple-element.11.own, f32[1,4,2,128,128]{4,3,2,1,0:T(8,128)S(1)} %get-tuple-element.12.early, f32[8,128]{1,0:T(8,128)S(1)} %get-tuple-element.14.token), custom_call_target="tpu_custom_call" | custom-call | tf_op jit(solution)/shard_map/pallas_call | solution.py:414
  60.4 2.0 %shard_map.53 = f32[4,2048,128]{2,1,0:T(8,128)} custom-call(f32[16,4,128,128]{3,2,1,0:T(8,128)S(1)} %get-tuple-element.10.last, f32[4,2,128,128]{3,2,1,0:T(8,128)S(1)} %get-tuple-element.11.own, f32[1,4,2,128,128]{4,3,2,1,0:T(8,128)S(1)} %get-tuple-element.15.others, f32[4,2048,128]{2,1,0:T(8,128)S(1)} %get-tuple-element.16.ready), custom_call_target="tpu_custom_call" | custom-call | tf_op jit(solution)/shard_map/pallas_call | solution.py:424
